TPU v7x, 512 devices: a 8x2x16 block of a 8x8x16 slice. The times are simulated.
512 devices in a mesh: job: 2 (over y), chain: 16 (over z), pair: 8 (over x), pno: 2 (over core).
Axes of the slice: x: 8, y: 2, z: 16, core: 2. Of those that a mesh axis runs over, the one named last changes fastest.
The devices are a block of a 8x8x16 slice.
Arguments:
- amplitudes: bfloat16 [1536, 128, 128], P(('job', 'chain', 'pair'), 'pno'), parts along dimension 0, may hold values from -4 to 4
- integrals: bfloat16 [1536, 128, 128], P(('job', 'chain', 'pair'), 'pno'), parts along dimension 0, may hold values from -6 to 6
- intersections: bfloat16 [1536, 32, 128, 128], P(('job', 'chain', 'pair')), parts along dimension 0, may hold values from -0.5 to 0.5
- coupling: float32 [1536, 32], P(('job', 'chain', 'pair')), parts along dimension 0, may hold values from -4 to 4
- pno_energies: float32 [1536, 128], P(('job', 'chain', 'pair')), parts along dimension 0, may hold values from 0.3 to 3
- pair_shift: float32 [1536], P(('job', 'chain', 'pair')), parts along dimension 0, may hold values from -1.5 to -0.3
- ranks: int32 [1536], P(('job', 'chain', 'pair')), parts along dimension 0, may hold values from 24 to 128
- neighbours: int32 [1536, 32], P(('job', 'chain', 'pair')), parts along dimension 0, may hold values from 0 to 767, as said below
Outputs:
- final_amplitudes: bfloat16 [1536, 128, 128], P(('job', 'chain', 'pair'), 'pno'), parts along dimension 0
- residual_norms: float32 [6], P('job'), parts along dimension 0
There are 2 independent parts, one for each index of `job`. A program takes and returns all parts, laid end to end along the dimension named above; each array names one. Nothing has to cross between parts.
Inputs may be any that keep to these rules, and one draw needn't show every extreme that they name: `neighbours`: every coupled pair of pair g lies in the fragment of g (pairs k * 48 to (k + 1) * 48 - 1 for k = g // 48) or in one of the two fragments beside it.
All inputs are finite; a program needn't handle non-finite values.
Results may differ from a plain program's by a relative error of at most 0.015.
Values may be sent and summed in bfloat16 or wider, within the bound.
No kernel may reach another device: no remote copies, remote signals or barrier semaphores. Data moves between devices by JAX's collectives and lax.ppermute only.
A program may use at most 64 MiB of HBM per device.

v0:
```python
import jax
import jax.numpy as jnp
from jax import lax
from jax.sharding import PartitionSpec as P

ITERS = 3


def laid_out(tiles, dim):
    tiles = jnp.moveaxis(tiles, 0, dim)
    shape = tiles.shape
    return tiles.reshape(*shape[:dim], shape[dim] * shape[dim + 1], *shape[dim + 2 :])


def copy_for_each(value, axis):
    copies = jnp.broadcast_to(value, (lax.axis_size(axis), *value.shape))
    return lax.all_to_all(copies, axis, split_axis=0, concat_axis=0, tiled=True)


def gathered_copies(value, axis, dim):
    return laid_out(copy_for_each(value, axis), dim)


def padded(cells, sides, width):
    for axis, dim in sides:
        count = lax.axis_size(axis)
        ends = count - 1
        head = lax.slice_in_dim(cells, 0, width, axis=dim)
        tail = lax.slice_in_dim(cells, cells.shape[dim] - width, cells.shape[dim], axis=dim)
        cells = jnp.concatenate(
            [
                lax.ppermute(tail, axis, [(i, (i + 1) % count) for i in range(ends)]),
                cells,
                lax.ppermute(head, axis, [((i + 1) % count, i) for i in range(ends)]),
            ],
            axis=dim,
        )
    return cells


def over_axes(value, axes):
    for axis in axes:
        value = lax.psum(value, axis)
    return value


def spread_amps(piece):
    whole_rows = gathered_copies(piece, "pno", 1)
    beside = padded(whole_rows, (("chain", 0),), whole_rows.shape[0])
    return lax.all_gather(beside, "pair", axis=0, tiled=True)


def per_device(
    amplitudes, integrals, intersections, coupling, pno_energies, pair_shift, ranks, neighbours
):
    count = amplitudes.shape[0]
    half = amplitudes.shape[1]
    width = amplitudes.shape[2]
    chain_pos = lax.axis_index("chain")
    first_row = lax.axis_index("pno") * half
    frag = count * lax.axis_size("pair")
    cells = frag * lax.axis_size("chain") * width * width
    columns = jnp.arange(width, dtype=jnp.int32)
    rows_here = first_row + jnp.arange(half, dtype=jnp.int32)
    live_cols = columns[None, :] < ranks[:, None]
    live_rows = rows_here[None, :] < ranks[:, None]
    mask = (live_rows[:, :, None] & live_cols[:, None, :]).astype(jnp.float32)
    energy_rows = lax.dynamic_slice_in_dim(pno_energies, first_row, half, 1)
    denom = energy_rows[:, :, None] + pno_energies[:, None, :] - pair_shift[:, None, None]
    over_rows = lax.dynamic_slice_in_dim(intersections, first_row, half, 2)
    own = (amplitudes.astype(jnp.float32) * mask).astype(jnp.bfloat16)
    ints = integrals.astype(jnp.float32)
    offset = neighbours // frag - chain_pos + 1
    within = neighbours % frag
    slots = within // count * (3 * count) + offset * count + within % count
    window = spread_amps(own)
    norms = []
    for step_no in range(ITERS):
        blocks = jnp.take(window, slots, axis=0)
        proj = jnp.einsum(
            "pnab,pnbc->pnac", over_rows, blocks, preferred_element_type=jnp.float32
        ).astype(jnp.bfloat16)
        terms = jnp.einsum(
            "pnac,pnbc->pnab", proj, intersections, preferred_element_type=jnp.float32
        )
        coupled = jnp.einsum("pn,pnab->pab", coupling, terms)
        own32 = own.astype(jnp.float32)
        resid = mask * (ints + coupled - denom * own32)
        delta = resid / denom
        more = step_no + 1 < ITERS
        squares = over_axes(jnp.sum(resid * resid), ("chain", "pair", "pno"))
        rms = jnp.sqrt(squares / cells)
        factor = 1.0 / (1.0 + rms)
        norms.append(rms)
        own = (own32 + delta * factor).astype(jnp.bfloat16)
        if more:
            window = spread_amps(own)
    return (own, jnp.stack(norms))


def solution(mesh):
    in_specs = (
        P(("job", "chain", "pair"), "pno", None),
        P(("job", "chain", "pair"), "pno", None),
        P(("job", "chain", "pair"), None, None, None),
        P(("job", "chain", "pair"), None),
        P(("job", "chain", "pair"), None),
        P(("job", "chain", "pair")),
        P(("job", "chain", "pair")),
        P(("job", "chain", "pair"), None),
    )
    out_specs = (P(("job", "chain", "pair"), "pno", None), P("job"))
    return jax.shard_map(
        per_device, mesh=mesh, in_specs=in_specs, out_specs=out_specs, check_vma=False
    )
```

profile of v0, /device:TPU:65, one launch (start us, length us, event | category | flops | bytes accessed | tf_op | source)
XLA Modules:
  0.0 529.5 jit_solution(2827774392820882856)
XLA Ops:
  7.3 0.7 iota_compare_fusion
  8.0 0.7 broadcast_compare_fusion
  8.7 1.0 fusion.48
  9.8 45.0 %all_to_all.15 = bf16[2,6,64,128]{3,2,1,0:T(8,128)(2,1)S(1)} all-to-all(bf16[2,6,64,128]{3,2,1,0:T(8,128)(2,1)S(1)} %broadcast_in_dim.12), channel_id=1, replica_groups=mesh['job'=2,'chain'=16,'pair'=8,'pno'=2] {'pno'}, dimensions={0} | all-to-all | bytes 393216 | tf_op jit(solution)/shard_map/all_to_all | solution.py:17
  54.8 1.3 collective-permute-start.1
  56.1 4.0 collective-permute-start
  60.1 2.7 collective-permute-done.1
  62.8 0.9 collective-permute-done
  63.7 0.9 pad_maximum_fusion
  64.7 0.7 compare_and_fusion
  65.6 0.8 constant_dynamic-slice_fusion
  66.3 58.9 %all-gather.4.cloned.1.call-done = bf16[144,128,128]{2,1,0:T(8,128)(2,1)} async-done(((bf16[18,128,128]{2,1,0:T(8,128)(2,1)}), bf16[144,128,128]{2,1,0:T(8,128)(2,1)}) %all-gather.4.cloned.1.call-update) | async-done | bytes 4718608 | tf_op jit(solution)/shard_map/all_gather | solution.py:50
  125.2 10.4 %gather_fusion = bf16[192,128,128]{2,1,0:T(8,128)(2,1)} fusion(bf16[144,128,128]{2,1,0:T(8,128)(2,1)} %all-gather.4.cloned.1.call-done, s32[1024]{0:T(1024)S(1)} %pad_clamp_fusion), kind=kCustom, calls=%fused_computation.clone | custom fusion | bytes 12583680 | tf_op jit(solution)/shard_map/jit(_take)/gather | solution.py:79
  135.6 10.9 %fusion.22 = bf16[6,32,64,128]{3,2,1,0:T(8,128)(2,1)} fusion(bf16[6,32,128,128]{3,2,1,0:T(8,128)(2,1)} %param.12, bf16[6,32,128,128]{3,2,1,0:T(8,128)(2,1)} %bitcast.29, pred[6,32]{1,0:T(8,128)(4,1)S(1)} %get-tuple-element.3, s32[]{:T(128)S(6)} %select_n.29), kind=kOutput, calls=%fused_computation.25 | convolution fusion | flops 810024960 | bytes 18874564 | tf_op jit(solution)/shard_map/pnac,pnbc->pnab/dot_general | solution.py:83
  146.5 3.7 fusion.4
  150.2 0.8 multiply_reduce_fusion.2
  151.0 25.8 %psum.63 = f32[]{:T(128)} all-reduce(f32[]{:T(128)} %multiply_reduce_fusion.2), channel_id=1, replica_groups=mesh['job'=2,'chain'=16,'pair'=8,'pno'=2] {'chain'}, use_global_device_ids=true, to_apply=%region_1.3 | all-reduce | flops 1 | bytes 8 | tf_op jit(solution)/shard_map/psum | solution.py:43
  176.7 12.7 %psum.64 = f32[]{:T(128)} all-reduce(f32[]{:T(128)} %psum.63), channel_id=1, replica_groups=mesh['job'=2,'chain'=16,'pair'=8,'pno'=2] {'pair'}, use_global_device_ids=true, to_apply=%region_2.4 | all-reduce | flops 1 | bytes 8 | tf_op jit(solution)/shard_map/psum | solution.py:43
  189.4 14.2 %psum.65 = f32[]{:T(128)} all-reduce(f32[]{:T(128)} %psum.64), channel_id=1, replica_groups=mesh['job'=2,'chain'=16,'pair'=8,'pno'=2] {'pno'}, use_global_device_ids=true, to_apply=%region_3.5 | all-reduce | flops 1 | bytes 8 | tf_op jit(solution)/shard_map/psum | solution.py:43
  204.6 3.9 all_to_all.16
  208.5 1.3 collective-permute-start.3
  209.8 4.0 collective-permute-start.2
  213.8 2.7 collective-permute-done.3
  216.5 0.9 collective-permute-done.2
  217.4 0.9 pad_maximum_fusion.1
  218.6 65.3 %all-gather.6.cloned.1.call-done = bf16[144,128,128]{2,1,0:T(8,128)(2,1)} async-done(((bf16[18,128,128]{2,1,0:T(8,128)(2,1)}), bf16[144,128,128]{2,1,0:T(8,128)(2,1)}) %all-gather.6.cloned.1.call-update) | async-done | bytes 4718608 | tf_op jit(solution)/shard_map/all_gather | solution.py:50
  283.9 10.4 %gather_fusion.1 = bf16[192,128,128]{2,1,0:T(8,128)(2,1)} fusion(bf16[144,128,128]{2,1,0:T(8,128)(2,1)} %all-gather.6.cloned.1.call-done, s32[1024]{0:T(1024)S(1)} %pad_clamp_fusion), kind=kCustom, calls=%fused_computation.1.clone | custom fusion | bytes 12583680 | tf_op jit(solution)/shard_map/jit(_take)/gather | solution.py:79
  294.3 10.8 %fusion.20 = bf16[6,32,64,128]{3,2,1,0:T(8,128)(2,1)} fusion(bf16[6,32,128,128]{3,2,1,0:T(8,128)(2,1)} %param.12, bf16[6,32,128,128]{3,2,1,0:T(8,128)(2,1)} %bitcast.30, pred[6,32]{1,0:T(8,128)(4,1)S(1)} %get-tuple-element.3, s32[]{:T(128)S(6)} %select_n.29), kind=kOutput, calls=%fused_computation.23 | convolution fusion | flops 810024960 | bytes 18874564 | tf_op jit(solution)/shard_map/pnac,pnbc->pnab/dot_general | solution.py:83
  305.1 3.7 fusion.2
  308.8 0.8 multiply_reduce_fusion.1
  309.6 25.8 %psum.66 = f32[]{:T(128)} all-reduce(f32[]{:T(128)} %multiply_reduce_fusion.1), channel_id=1, replica_groups=mesh['job'=2,'chain'=16,'pair'=8,'pno'=2] {'chain'}, use_global_device_ids=true, to_apply=%region_5.7 | all-reduce | flops 1 | bytes 8 | tf_op jit(solution)/shard_map/psum | solution.py:43
  335.4 12.7 %psum.67 = f32[]{:T(128)} all-reduce(f32[]{:T(128)} %psum.66), channel_id=1, replica_groups=mesh['job'=2,'chain'=16,'pair'=8,'pno'=2] {'pair'}, use_global_device_ids=true, to_apply=%region_6.8 | all-reduce | flops 1 | bytes 8 | tf_op jit(solution)/shard_map/psum | solution.py:43
  348.0 14.2 %psum.68 = f32[]{:T(128)} all-reduce(f32[]{:T(128)} %psum.67), channel_id=1, replica_groups=mesh['job'=2,'chain'=16,'pair'=8,'pno'=2] {'pno'}, use_global_device_ids=true, to_apply=%region_7.9 | all-reduce | flops 1 | bytes 8 | tf_op jit(solution)/shard_map/psum | solution.py:43
  363.2 3.9 all_to_all.17
  367.1 1.3 collective-permute-start.5
  368.4 4.3 collective-permute-start.4
  372.7 2.4 collective-permute-done.5
  375.1 0.9 collective-permute-done.4
  376.1 0.9 pad_maximum_fusion.2
  377.0 65.5 %all-gather.8.cloned.1.call-done = bf16[144,128,128]{2,1,0:T(8,128)(2,1)} async-done(((bf16[18,128,128]{2,1,0:T(8,128)(2,1)}), bf16[144,128,128]{2,1,0:T(8,128)(2,1)}) %all-gather.8.cloned.1.call-update) | async-done | bytes 4718608 | tf_op jit(solution)/shard_map/all_gather | solution.py:50
  442.5 10.4 %gather_fusion.2 = bf16[192,128,128]{2,1,0:T(8,128)(2,1)} fusion(bf16[144,128,128]{2,1,0:T(8,128)(2,1)} %all-gather.8.cloned.1.call-done, s32[1024]{0:T(1024)S(1)} %pad_clamp_fusion), kind=kCustom, calls=%fused_computation.2.clone | custom fusion | bytes 12583680 | tf_op jit(solution)/shard_map/jit(_take)/gather | solution.py:79
  452.9 10.8 %fusion.18 = bf16[6,32,64,128]{3,2,1,0:T(8,128)(2,1)} fusion(bf16[6,32,128,128]{3,2,1,0:T(8,128)(2,1)} %param.12, bf16[6,32,128,128]{3,2,1,0:T(8,128)(2,1)} %bitcast.28, pred[6,32]{1,0:T(8,128)(4,1)S(1)} %get-tuple-element.3, s32[]{:T(128)S(6)} %select_n.29), kind=kOutput, calls=%fused_computation.21 | convolution fusion | flops 810024960 | bytes 18874564 | tf_op jit(solution)/shard_map/pnac,pnbc->pnab/dot_general | solution.py:83
  463.7 3.7 fusion
  467.5 0.8 multiply_reduce_fusion
  468.2 26.0 %psum.69 = f32[]{:T(128)} all-reduce(f32[]{:T(128)} %multiply_reduce_fusion), channel_id=1, replica_groups=mesh['job'=2,'chain'=16,'pair'=8,'pno'=2] {'chain'}, use_global_device_ids=true, to_apply=%region_9.11 | all-reduce | flops 1 | bytes 8 | tf_op jit(solution)/shard_map/psum | solution.py:43
  494.2 12.5 %psum.70 = f32[]{:T(128)} all-reduce(f32[]{:T(128)} %psum.69), channel_id=1, replica_groups=mesh['job'=2,'chain'=16,'pair'=8,'pno'=2] {'pair'}, use_global_device_ids=true, to_apply=%region_10.12 | all-reduce | flops 1 | bytes 8 | tf_op jit(solution)/shard_map/psum | solution.py:43
  506.7 14.2 %psum.71 = f32[]{:T(128)} all-reduce(f32[]{:T(128)} %psum.70), channel_id=1, replica_groups=mesh['job'=2,'chain'=16,'pair'=8,'pno'=2] {'pno'}, use_global_device_ids=true, to_apply=%region_11.13 | all-reduce | flops 1 | bytes 8 | tf_op jit(solution)/shard_map/psum | solution.py:43
  521.6 0.8 fusion.47
  (28 shorter events, 1.7 us)
Async XLA Ops:
  7.2 139.3 %copy-start = (f32[6,32]{1,0:T(8,128)S(1)}, f32[6,32]{1,0:T(8,128)}, u32[]{:S(2)}) copy-start(f32[6,32]{1,0:T(8,128)} %param.13) | copy-start | bytes 2308
  7.2 118.0 %all-gather.4.cloned.1.call-start = ((), (), s32[]{:S(2)}) async-start(), calls=%async_computation.3 | async-start | bytes 5308416 | tf_op jit(solution)/shard_map/all_gather | solution.py:50
  54.8 8.0 %collective-permute-start.1 = (bf16[6,128,128]{2,1,0:T(8,128)(2,1)S(1)}, bf16[6,128,128]{2,1,0:T(8,128)(2,1)S(1)}, u32[]{:S(2)}, u32[]{:S(2)}) collective-permute-start(bf16[6,128,128]{2,1,0:T(8,128)(2,1)S(1)} %bitcast.31), channel_id=1, source_target_pairs={{16,0},{32,16},{48,32},{64,48},{80,64},{96,80},{112,96},{128,112},... | collective-permute-start | bytes 589832 | tf_op jit(solution)/shard_map/ppermute | solution.py:34
  56.1 7.6 %collective-permute-start = (bf16[6,128,128]{2,1,0:T(8,128)(2,1)S(1)}, bf16[6,128,128]{2,1,0:T(8,128)(2,1)S(1)}, u32[]{:S(2)}, u32[]{:S(2)}) collective-permute-start(bf16[6,128,128]{2,1,0:T(8,128)(2,1)S(1)} %bitcast.32), channel_id=1, source_target_pairs={{0,16},{16,32},{32,48},{48,64},{64,80},{80,96},{96,112},{112,128},... | collective-permute-start | bytes 589832 | tf_op jit(solution)/shard_map/ppermute | solution.py:32
  64.7 219.2 %all-gather.6.cloned.1.call-start = ((), (), s32[]{:S(2)}) async-start(), calls=%async_computation.4 | async-start | bytes 5308416 | tf_op jit(solution)/shard_map/all_gather | solution.py:50
  135.6 14.6 %copy-start.1 = (bf16[6,64,128]{2,1,0:T(8,128)(2,1)S(1)}, bf16[6,64,128]{2,1,0:T(8,128)(2,1)}, u32[]{:S(2)}) copy-start(bf16[6,64,128]{2,1,0:T(8,128)(2,1)} %param.11) | copy-start | bytes 294916
  135.6 14.6 %copy-start.2 = (bf16[6,64,128]{2,1,0:T(8,128)(2,1)S(1)}, bf16[6,64,128]{2,1,0:T(8,128)(2,1)}, u32[]{:S(2)}) copy-start(bf16[6,64,128]{2,1,0:T(8,128)(2,1)} %param.10) | copy-start | bytes 294916
  135.6 14.6 %copy-start.3 = (f32[6,128]{1,0:T(8,128)S(1)}, f32[6,128]{1,0:T(8,128)}, u32[]{:S(2)}) copy-start(f32[6,128]{1,0:T(8,128)} %param.14) | copy-start | bytes 9220
  135.6 14.6 %copy-start.4 = (f32[6]{0:T(128)S(1)}, f32[6]{0:T(128)}, u32[]{:S(2)}) copy-start(f32[6]{0:T(128)} %param.15) | copy-start | bytes 76
  208.5 8.0 %collective-permute-start.3 = (bf16[6,128,128]{2,1,0:T(8,128)(2,1)S(1)}, bf16[6,128,128]{2,1,0:T(8,128)(2,1)S(1)}, u32[]{:S(2)}, u32[]{:S(2)}) collective-permute-start(bf16[6,128,128]{2,1,0:T(8,128)(2,1)S(1)} %bitcast.34), channel_id=1, source_target_pairs={{16,0},{32,16},{48,32},{64,48},{80,64},{96,80},{112,96},{128,112},... | collective-permute-start | bytes 589832 | tf_op jit(solution)/shard_map/ppermute | solution.py:34
  209.8 7.6 %collective-permute-start.2 = (bf16[6,128,128]{2,1,0:T(8,128)(2,1)S(1)}, bf16[6,128,128]{2,1,0:T(8,128)(2,1)S(1)}, u32[]{:S(2)}, u32[]{:S(2)}) collective-permute-start(bf16[6,128,128]{2,1,0:T(8,128)(2,1)S(1)} %bitcast.35), channel_id=1, source_target_pairs={{0,16},{16,32},{32,48},{48,64},{64,80},{80,96},{96,112},{112,128},... | collective-permute-start | bytes 589832 | tf_op jit(solution)/shard_map/ppermute | solution.py:32
  218.4 224.2 %all-gather.8.cloned.1.call-start = ((), (), s32[]{:S(2)}) async-start(), calls=%async_computation.5 | async-start | bytes 5308416 | tf_op jit(solution)/shard_map/all_gather | solution.py:50
  367.1 8.0 %collective-permute-start.5 = (bf16[6,128,128]{2,1,0:T(8,128)(2,1)S(1)}, bf16[6,128,128]{2,1,0:T(8,128)(2,1)S(1)}, u32[]{:S(2)}, u32[]{:S(2)}) collective-permute-start(bf16[6,128,128]{2,1,0:T(8,128)(2,1)S(1)} %bitcast.37), channel_id=1, source_target_pairs={{16,0},{32,16},{48,32},{64,48},{80,64},{96,80},{112,96},{128,112},... | collective-permute-start | bytes 589832 | tf_op jit(solution)/shard_map/ppermute | solution.py:34
  368.4 7.6 %collective-permute-start.4 = (bf16[6,128,128]{2,1,0:T(8,128)(2,1)S(1)}, bf16[6,128,128]{2,1,0:T(8,128)(2,1)S(1)}, u32[]{:S(2)}, u32[]{:S(2)}) collective-permute-start(bf16[6,128,128]{2,1,0:T(8,128)(2,1)S(1)} %bitcast.38), channel_id=1, source_target_pairs={{0,16},{16,32},{32,48},{48,64},{64,80},{80,96},{96,112},{112,128},... | collective-permute-start | bytes 589832 | tf_op jit(solution)/shard_map/ppermute | solution.py:32
Sparse Core Ops, SparseCore 0:
  64.8 60.3 all-gather.3
  218.5 65.3 all-gather.5
  377.1 65.3 all-gather.7
where the time goes:
time: 530 us
  blocking collectives  211 us (40%)
  waiting for transfers between devices  200 us (38%)
  matrix products  43.6 us (8%)
  local copies, waits for them, and re-layouts  32.2 us (6%)
  starting transfers between devices  16.6 us (3%)
  between operations  16.1 us (3%)
  other arithmetic  9.94 us (2%)
    all_gather x3, waiting for transfers between devices, spread_amps(): return lax.all_gather(beside, 'pair', axis=0, tiled=True)  190 us
    psum x9, blocking collectives, over_axes(): value = lax.psum(value, axis)  158 us
    all_to_all x3, blocking collectives, copy_for_each(): return lax.all_to_all(copies, axis, split_axis=0, concat_axis=0, tiled=True)  52.8 us
    dot_general x3, matrix products, per_device(): jnp.einsum('pnac,pnbc->pnab', proj, intersections, preferred_element_type...  32.5 us
    gather x3, local copies, waits for them, and re-layouts, per_device(): blocks = jnp.take(window, slots, axis=0)  31.2 us
    ppermute x3, starting transfers between devices, padded(): lax.ppermute(tail, axis, [(i, (i + 1) % count) for i in range(ends)])  12.4 us
    dot_general x3, matrix products, per_device(): coupled = jnp.einsum('pn,pnab->pab', coupling, terms)  11.2 us
  transfers between devices with their start and end apart: 9, of which 9 were waited for; matrix products, arithmetic and copies ran while one was open for 0% of the time, Pallas kernels for 0%

commit v1 on v0

--- a/solution.py
+++ b/solution.py
@@ -4,6 +4,13 @@
 from jax.sharding import PartitionSpec as P
 
 ITERS = 3
+
+
+def _apply_fields(mine):
+    value_now = tuple((mine for _ in range(lax.axis_size("pair"))))
+    carry = jnp.concatenate(value_now, axis=0)
+    w1 = lax.all_to_all(carry, "pair", 0, 0, tiled=True)
+    return w1
 
 
 def laid_out(tiles, dim):
@@ -47,7 +54,7 @@
 def spread_amps(piece):
     whole_rows = gathered_copies(piece, "pno", 1)
     beside = padded(whole_rows, (("chain", 0),), whole_rows.shape[0])
-    return lax.all_gather(beside, "pair", axis=0, tiled=True)
+    return _apply_fields(beside)
 
 
 def per_device(

time: 530 us -> 669 us (1.26)
  blocking collectives: 211 us -> 424 us
  waiting for transfers between devices: 200 us -> 126 us
  local copies, waits for them, and re-layouts: 32.2 us -> 49.3 us
  between operations: 16.1 us -> 3.35 us
    all_to_all x0 -> x2, blocking collectives: none -> 217 us  [_apply_fields(): w1 = lax.all_to_all(carry, 'pair', 0, 0, tiled=True)]
    all_gather x3 -> x0, waiting for transfers between devices: 190 us -> none  [spread_amps(): return lax.all_gather(beside, 'pair', axis=0, tiled=True)]
    all_to_all x0 -> x1, waiting for transfers between devices: none -> 108 us  [_apply_fields(): w1 = lax.all_to_all(carry, 'pair', 0, 0, tiled=True)]
    unnamed x10 -> x81, local copies, waits for them, and re-layouts: 0.02 us -> 17.1 us
  transfers between devices with their start and end apart: 9 -> 7, of which waited for: 9 -> 7; matrix products, arithmetic and copies ran while one was open for 0% -> 0% of each run, Pallas kernels for 0% -> 0%
where the time goes in v1:
time: 669 us; the launch traced here: 668 us
  blocking collectives  424 us (63%)
  waiting for transfers between devices  126 us (19%)
  local copies, waits for them, and re-layouts  49.3 us (7%)
  matrix products  43.6 us (7%)
  starting transfers between devices  14.6 us (2%)
    all_to_all x2, blocking collectives, _apply_fields(): w1 = lax.all_to_all(carry, 'pair', 0, 0, tiled=True)  217 us
    psum x9, blocking collectives, over_axes(): value = lax.psum(value, axis)  155 us
    all_to_all x1, waiting for transfers between devices, _apply_fields(): w1 = lax.all_to_all(carry, 'pair', 0, 0, tiled=True)  108 us
    all_to_all x3, blocking collectives, copy_for_each(): return lax.all_to_all(copies, axis, split_axis=0, concat_axis=0, tiled=True)  52.8 us
    dot_general x3, matrix products, per_device(): jnp.einsum('pnac,pnbc->pnab', proj, intersections, preferred_element_type...  32.4 us
    gather x3, local copies, waits for them, and re-layouts, per_device(): blocks = jnp.take(window, slots, axis=0)  31.2 us
    unnamed x81, local copies, waits for them, and re-layouts  17.1 us
  transfers between devices with their start and end apart: 7, of which 7 were waited for; matrix products, arithmetic and copies ran while one was open for 0% of the time, Pallas kernels for 0%

profile of v1, /device:TPU:65, one launch (start us, length us, event | category | flops | bytes accessed | tf_op | source)
XLA Modules:
  0.0 667.6 jit_solution(1467421379075168891)
XLA Ops:
  0.7 0.7 iota_compare_fusion
  1.4 0.7 broadcast_compare_fusion
  2.1 1.0 fusion.48
  3.2 45.0 %all_to_all.30 = bf16[2,6,64,128]{3,2,1,0:T(8,128)(2,1)S(1)} all-to-all(bf16[2,6,64,128]{3,2,1,0:T(8,128)(2,1)S(1)} %broadcast_in_dim.12), channel_id=1, replica_groups=mesh['job'=2,'chain'=16,'pair'=8,'pno'=2] {'pno'}, dimensions={0} | all-to-all | bytes 393216 | tf_op jit(solution)/shard_map/all_to_all | solution.py:24
  48.2 1.3 collective-permute-start
  49.5 1.3 collective-permute-start.1
  50.8 2.8 collective-permute-done
  55.0 2.5 collective-permute-done.1
  60.9 0.7 constant_dynamic-update-slice_fusion.16
  63.7 0.7 constant_dynamic-update-slice_fusion.12
  66.4 0.7 constant_dynamic-update-slice_fusion.8
  67.1 0.7 constant_dynamic-update-slice_fusion.7
  72.6 4.9 all-to-all-start.1
  77.8 107.8 %all-to-all-done.1 = bf16[144,128,128]{2,1,0:T(8,128)(2,1)} async-done(((bf16[144,128,128]{2,1,0:T(8,128)(2,1)}), bf16[144,128,128]{2,1,0:T(8,128)(2,1)}, u32[]{:S(2)}, u32[]{:S(2)}) %all-to-all-start.1) | async-done | bytes 4718624 | tf_op jit(solution)/shard_map/all_to_all | solution.py:12
  185.6 10.4 %gather_fusion = bf16[192,128,128]{2,1,0:T(8,128)(2,1)} fusion(bf16[144,128,128]{2,1,0:T(8,128)(2,1)} %all-to-all-done.1, s32[1024]{0:T(1024)S(1)} %pad_clamp_fusion), kind=kCustom, calls=%fused_computation.clone | custom fusion | bytes 12583680 | tf_op jit(solution)/shard_map/jit(_take)/gather | solution.py:86
  196.0 10.8 %fusion.22 = bf16[6,32,64,128]{3,2,1,0:T(8,128)(2,1)} fusion(bf16[6,32,128,128]{3,2,1,0:T(8,128)(2,1)} %param.12, bf16[6,32,128,128]{3,2,1,0:T(8,128)(2,1)} %bitcast.59, pred[6,32]{1,0:T(8,128)(4,1)S(1)} %get-tuple-element.3, s32[]{:T(128)S(6)} %select_n.29), kind=kOutput, calls=%fused_computation.25 | convolution fusion | flops 810024960 | bytes 18874564 | tf_op jit(solution)/shard_map/pnac,pnbc->pnab/dot_general | solution.py:90
  206.8 3.7 fusion.4
  210.5 0.8 multiply_reduce_fusion.2
  211.3 25.0 %psum.63 = f32[]{:T(128)} all-reduce(f32[]{:T(128)} %multiply_reduce_fusion.2), channel_id=1, replica_groups=mesh['job'=2,'chain'=16,'pair'=8,'pno'=2] {'chain'}, use_global_device_ids=true, to_apply=%region_1.3 | all-reduce | flops 1 | bytes 8 | tf_op jit(solution)/shard_map/psum | solution.py:50
  236.3 11.4 %psum.64 = f32[]{:T(128)} all-reduce(f32[]{:T(128)} %psum.63), channel_id=1, replica_groups=mesh['job'=2,'chain'=16,'pair'=8,'pno'=2] {'pair'}, use_global_device_ids=true, to_apply=%region_2.4 | all-reduce | flops 1 | bytes 8 | tf_op jit(solution)/shard_map/psum | solution.py:50
  247.7 14.2 %psum.65 = f32[]{:T(128)} all-reduce(f32[]{:T(128)} %psum.64), channel_id=1, replica_groups=mesh['job'=2,'chain'=16,'pair'=8,'pno'=2] {'pno'}, use_global_device_ids=true, to_apply=%region_3.5 | all-reduce | flops 1 | bytes 8 | tf_op jit(solution)/shard_map/psum | solution.py:50
  262.9 3.9 all_to_all.31
  266.8 2.5 collective-permute-start.2
  269.3 1.3 collective-permute-start.3
  270.6 2.6 collective-permute-done.2
  273.2 3.8 collective-permute-done.3
  277.8 108.2 %all_to_all.32 = bf16[144,128,128]{2,1,0:T(8,128)(2,1)} all-to-all(bf16[144,128,128]{2,1,0:T(8,128)(2,1)S(1)} %constant_dynamic-update-slice_fusion.24), channel_id=1, replica_groups=mesh['job'=2,'chain'=16,'pair'=8,'pno'=2] {'pair'}, dimensions={0} | all-to-all | bytes 9437184 | tf_op jit(solution)/shard_map/all_to_all | solution.py:12
  386.0 10.4 %gather_fusion.1 = bf16[192,128,128]{2,1,0:T(8,128)(2,1)} fusion(bf16[144,128,128]{2,1,0:T(8,128)(2,1)} %all_to_all.32, s32[1024]{0:T(1024)S(1)} %pad_clamp_fusion), kind=kCustom, calls=%fused_computation.1.clone | custom fusion | bytes 12583680 | tf_op jit(solution)/shard_map/jit(_take)/gather | solution.py:86
  396.4 10.8 %fusion.20 = bf16[6,32,64,128]{3,2,1,0:T(8,128)(2,1)} fusion(bf16[6,32,128,128]{3,2,1,0:T(8,128)(2,1)} %param.12, bf16[6,32,128,128]{3,2,1,0:T(8,128)(2,1)} %bitcast.60, pred[6,32]{1,0:T(8,128)(4,1)S(1)} %get-tuple-element.3, s32[]{:T(128)S(6)} %select_n.29), kind=kOutput, calls=%fused_computation.23 | convolution fusion | flops 810024960 | bytes 18874564 | tf_op jit(solution)/shard_map/pnac,pnbc->pnab/dot_general | solution.py:90
  407.2 3.7 fusion.2
  411.0 0.8 multiply_reduce_fusion.1
  411.7 22.4 %psum.66 = f32[]{:T(128)} all-reduce(f32[]{:T(128)} %multiply_reduce_fusion.1), channel_id=1, replica_groups=mesh['job'=2,'chain'=16,'pair'=8,'pno'=2] {'chain'}, use_global_device_ids=true, to_apply=%region_5.7 | all-reduce | flops 1 | bytes 8 | tf_op jit(solution)/shard_map/psum | solution.py:50
  434.1 12.0 %psum.67 = f32[]{:T(128)} all-reduce(f32[]{:T(128)} %psum.66), channel_id=1, replica_groups=mesh['job'=2,'chain'=16,'pair'=8,'pno'=2] {'pair'}, use_global_device_ids=true, to_apply=%region_6.8 | all-reduce | flops 1 | bytes 8 | tf_op jit(solution)/shard_map/psum | solution.py:50
  446.1 16.6 %psum.68 = f32[]{:T(128)} all-reduce(f32[]{:T(128)} %psum.67), channel_id=1, replica_groups=mesh['job'=2,'chain'=16,'pair'=8,'pno'=2] {'pno'}, use_global_device_ids=true, to_apply=%region_7.9 | all-reduce | flops 1 | bytes 8 | tf_op jit(solution)/shard_map/psum | solution.py:50
  463.7 3.9 all_to_all.33
  467.6 1.9 collective-permute-start.4
  469.5 1.3 collective-permute-start.5
  470.9 2.6 collective-permute-done.4
  473.5 3.8 collective-permute-done.5
  478.1 108.3 %all_to_all.34 = bf16[144,128,128]{2,1,0:T(8,128)(2,1)} all-to-all(bf16[144,128,128]{2,1,0:T(8,128)(2,1)S(1)} %constant_dynamic-update-slice_fusion.48), channel_id=1, replica_groups=mesh['job'=2,'chain'=16,'pair'=8,'pno'=2] {'pair'}, dimensions={0} | all-to-all | bytes 9437184 | tf_op jit(solution)/shard_map/all_to_all | solution.py:12
  586.4 10.4 %gather_fusion.2 = bf16[192,128,128]{2,1,0:T(8,128)(2,1)} fusion(bf16[144,128,128]{2,1,0:T(8,128)(2,1)} %all_to_all.34, s32[1024]{0:T(1024)S(1)} %pad_clamp_fusion), kind=kCustom, calls=%fused_computation.2.clone | custom fusion | bytes 12583680 | tf_op jit(solution)/shard_map/jit(_take)/gather | solution.py:86
  596.8 10.8 %fusion.18 = bf16[6,32,64,128]{3,2,1,0:T(8,128)(2,1)} fusion(bf16[6,32,128,128]{3,2,1,0:T(8,128)(2,1)} %param.12, bf16[6,32,128,128]{3,2,1,0:T(8,128)(2,1)} %bitcast.58, pred[6,32]{1,0:T(8,128)(4,1)S(1)} %get-tuple-element.3, s32[]{:T(128)S(6)} %select_n.29), kind=kOutput, calls=%fused_computation.21 | convolution fusion | flops 810024960 | bytes 18874564 | tf_op jit(solution)/shard_map/pnac,pnbc->pnab/dot_general | solution.py:90
  607.6 3.7 fusion
  611.3 0.8 multiply_reduce_fusion
  612.1 24.7 %psum.69 = f32[]{:T(128)} all-reduce(f32[]{:T(128)} %multiply_reduce_fusion), channel_id=1, replica_groups=mesh['job'=2,'chain'=16,'pair'=8,'pno'=2] {'chain'}, use_global_device_ids=true, to_apply=%region_9.11 | all-reduce | flops 1 | bytes 8 | tf_op jit(solution)/shard_map/psum | solution.py:50
  636.8 12.1 %psum.70 = f32[]{:T(128)} all-reduce(f32[]{:T(128)} %psum.69), channel_id=1, replica_groups=mesh['job'=2,'chain'=16,'pair'=8,'pno'=2] {'pair'}, use_global_device_ids=true, to_apply=%region_10.12 | all-reduce | flops 1 | bytes 8 | tf_op jit(solution)/shard_map/psum | solution.py:50
  648.9 16.6 %psum.71 = f32[]{:T(128)} all-reduce(f32[]{:T(128)} %psum.70), channel_id=1, replica_groups=mesh['job'=2,'chain'=16,'pair'=8,'pno'=2] {'pno'}, use_global_device_ids=true, to_apply=%region_11.13 | all-reduce | flops 1 | bytes 8 | tf_op jit(solution)/shard_map/psum | solution.py:50
  666.2 0.8 fusion.47
  (94 shorter events, 16.3 us)
Async XLA Ops:
  0.6 206.2 %copy-start = (f32[6,32]{1,0:T(8,128)S(1)}, f32[6,32]{1,0:T(8,128)}, u32[]{:S(2)}) copy-start(f32[6,32]{1,0:T(8,128)} %param.13) | copy-start | bytes 2308
  48.2 5.5 collective-permute-start
  49.5 8.0 %collective-permute-start.1 = (bf16[6,128,128]{2,1,0:T(8,128)(2,1)S(1)}, bf16[6,128,128]{2,1,0:T(8,128)(2,1)S(1)}, u32[]{:S(2)}, u32[]{:S(2)}) collective-permute-start(bf16[6,128,128]{2,1,0:T(8,128)(2,1)S(1)} %bitcast.29), channel_id=1, source_target_pairs={{16,0},{32,16},{48,32},{64,48},{80,64},{96,80},{112,96},{128,112},... | collective-permute-start | bytes 589832 | tf_op jit(solution)/shard_map/ppermute | solution.py:41
  72.6 4.9 copy-start.5
  72.6 5.1 copy-start.3
  72.6 112.9 %all-to-all-start.1 = ((bf16[144,128,128]{2,1,0:T(8,128)(2,1)}), bf16[144,128,128]{2,1,0:T(8,128)(2,1)}, u32[]{:S(2)}, u32[]{:S(2)}) async-start(bf16[144,128,128]{2,1,0:T(8,128)(2,1)} %constant_dynamic-update-slice_fusion), calls=%async_computation.1 | async-start | bytes 9437184 | tf_op jit(solution)/shard_map/all_to_all | solution.py:12
  196.0 14.6 %copy-start.1 = (bf16[6,64,128]{2,1,0:T(8,128)(2,1)S(1)}, bf16[6,64,128]{2,1,0:T(8,128)(2,1)}, u32[]{:S(2)}) copy-start(bf16[6,64,128]{2,1,0:T(8,128)(2,1)} %param.11) | copy-start | bytes 294916
  196.0 14.6 %copy-start.2 = (bf16[6,64,128]{2,1,0:T(8,128)(2,1)S(1)}, bf16[6,64,128]{2,1,0:T(8,128)(2,1)}, u32[]{:S(2)}) copy-start(bf16[6,64,128]{2,1,0:T(8,128)(2,1)} %param.10) | copy-start | bytes 294916
  196.0 14.6 %copy-start.4 = (f32[6]{0:T(128)S(1)}, f32[6]{0:T(128)}, u32[]{:S(2)}) copy-start(f32[6]{0:T(128)} %param.15) | copy-start | bytes 76
  266.8 6.4 collective-permute-start.2
  269.3 7.7 %collective-permute-start.3 = (bf16[6,128,128]{2,1,0:T(8,128)(2,1)S(1)}, bf16[6,128,128]{2,1,0:T(8,128)(2,1)S(1)}, u32[]{:S(2)}, u32[]{:S(2)}) collective-permute-start(bf16[6,128,128]{2,1,0:T(8,128)(2,1)S(1)} %bitcast.39), channel_id=1, source_target_pairs={{16,0},{32,16},{48,32},{64,48},{80,64},{96,80},{112,96},{128,112},... | collective-permute-start | bytes 589832 | tf_op jit(solution)/shard_map/ppermute | solution.py:41
  467.6 5.8 collective-permute-start.4
  469.5 7.7 %collective-permute-start.5 = (bf16[6,128,128]{2,1,0:T(8,128)(2,1)S(1)}, bf16[6,128,128]{2,1,0:T(8,128)(2,1)S(1)}, u32[]{:S(2)}, u32[]{:S(2)}) collective-permute-start(bf16[6,128,128]{2,1,0:T(8,128)(2,1)S(1)} %bitcast.49), channel_id=1, source_target_pairs={{16,0},{32,16},{48,32},{64,48},{80,64},{96,80},{112,96},{128,112},... | collective-permute-start | bytes 589832 | tf_op jit(solution)/shard_map/ppermute | solution.py:41
